TPU v7x, 128 devices: a whole 4x4x4 slice. The times are simulated.
128 devices in a mesh: dp: 32 (over z, y, core), mp: 4 (over x).
Axes of the slice: x: 4, y: 4, z: 4, core: 2. Of those that a mesh axis runs over, the one named last changes fastest.
Arguments:
- ids: int32 [32768], P('dp'), may hold values from 0 to 16777215, as said below
- hash_a: int32 [1024], replicated, may hold values from 1 to 16383
- hash_b: int32 [1024], replicated, may hold values from 0 to 16383
- hash_p: int32 [1024], replicated, may hold values from 16384 to 32767
- hash_m: int32 [1024], replicated, may hold values from 4096 to 16383
- w_in: bfloat16 [1024, 2048], P(None, 'mp'), may hold values from -0.1875 to 0.1875
- w_mid: bfloat16 [2, 2048, 2048], P(None, None, 'mp'), may hold values from -0.125 to 0.125
- w_out: bfloat16 [2048, 64], P('mp'), may hold values from -0.125 to 0.125
- bn_gain: float32 [3, 2048], P(None, 'mp'), may hold values from 0.25 to 1.75
- bn_bias: float32 [3, 2048], P(None, 'mp'), may hold values from -3 to 3
- target: float32 [32768, 64], P('dp'), may hold values from -6 to 6
Outputs:
- grad_w_in: float32 [1024, 2048], P('dp', 'mp')
- grad_w_mid: float32 [2, 2048, 2048], P(None, 'dp', 'mp')
- grad_w_out: float32 [2048, 64], P(('mp', 'dp'))
- grad_gain: float32 [3, 2048], P(None, 'mp')
- grad_bias: float32 [3, 2048], P(None, 'mp')
Inputs may be any that keep to these rules, and one draw needn't show every extreme that they name: The number of distinct ids among one device's 1024 rows differs from device to device, from one to many.
All inputs are finite; a program needn't handle non-finite values.
Results may differ from a plain program's by a relative error of at most 0.02.
Values may be sent and summed in bfloat16 or wider, within the bound.
No kernel may reach another device: no remote copies, remote signals or barrier semaphores. Data moves between devices by JAX's collectives and lax.ppermute only.
A program may use at most 128 MiB of HBM per device.

v0:
```python
import math

import jax
import jax.numpy as jnp
from jax import lax
from jax.sharding import PartitionSpec as P

epsilon_norm = 1e-05


def from_everyone(array, axis):
    size = lax.axis_size(axis)
    return lax.all_to_all(
        jnp.broadcast_to(array[None], (size, *array.shape)), axis, 0, 0, tiled=True
    )


def over_copies(array, axis):
    everything = from_everyone(array, axis)
    return jnp.sum(everything, axis=0)


def together(arrays, axis):
    ends = [0]
    for a in arrays:
        ends.append(ends[-1] + a.size)
    total = over_copies(jnp.concatenate([a.ravel() for a in arrays]), axis)
    return tuple((total[b:e].reshape(a.shape) for a, b, e in zip(arrays, ends, ends[1:])))


def of_everyone(array, axis):
    everything = from_everyone(array, axis)
    return jnp.sum(everything.astype(jnp.float32), axis=0)


def cut_along(array, dim, size):
    dims = array.shape
    parts = array.reshape(*dims[:dim], size, dims[dim] // size, *dims[dim + 1 :])
    return jnp.moveaxis(parts, dim, 0)


def sum_at_owner(array, axis, dim):
    size = lax.axis_size(axis)
    parts = lax.all_to_all(cut_along(array, dim, size), axis, 0, 0, tiled=True)
    return jnp.sum(parts.astype(jnp.float32), axis=0)


def encode(ids, hash_a, hash_b, hash_p, hash_m):
    reduced = ids[:, None] % hash_p[None, :]
    hashed = (hash_a[None, :] * reduced + hash_b[None, :]) % hash_p[None, :] % hash_m[None, :]
    scaled = 2.0 * hashed.astype(jnp.float32) / (hash_m[None, :] - 1).astype(jnp.float32) - 1.0
    return scaled.astype(jnp.bfloat16)


def mish_act(values):
    return values * jnp.tanh(jax.nn.softplus(values))


def mish_slope(values):
    tangent = jnp.tanh(jax.nn.softplus(values))
    return tangent + values * (1.0 - tangent * tangent) * jax.nn.sigmoid(values)


def column_stats(summed, batch_total):
    totals, squares = together((jnp.sum(summed, axis=0), jnp.sum(summed * summed, axis=0)), "dp")
    average = totals / batch_total
    spread = squares / batch_total - average * average
    centered = summed - average
    inverse = 1.0 / jnp.sqrt(spread + epsilon_norm)
    return (centered * inverse, inverse)


def column_products(left_rows, right_rows):
    return jnp.dot(left_rows.T, right_rows, preferred_element_type=jnp.float32)


def per_device(ids, hash_a, hash_b, hash_p, hash_m, w_in, w_mid, w_out, bn_gain, bn_bias, target):
    batch_devices = lax.axis_size("dp")
    batch_total = ids.shape[0] * batch_devices
    layer_count = bn_gain.shape[0]
    encoded = encode(ids, hash_a, hash_b, hash_p, hash_m)
    full_inputs = []
    saved = []
    current = encoded
    for layer_at in range(layer_count):
        if layer_at == 0:
            whole_input = encoded
            summed = jnp.dot(whole_input, w_in, preferred_element_type=jnp.float32)
        else:
            whole_input = lax.all_gather(current, "mp", axis=1, tiled=True)
            summed = jnp.dot(whole_input, w_mid[layer_at - 1], preferred_element_type=jnp.float32)
        full_inputs.append(whole_input)
        normed, inverse = column_stats(summed, batch_total)
        shifted = bn_gain[layer_at] * normed + bn_bias[layer_at]
        current = mish_act(shifted).astype(jnp.bfloat16)
        saved.append((normed, inverse, shifted))
    partial_out = jnp.dot(current, w_out, preferred_element_type=jnp.float32)
    predicted = of_everyone(partial_out.astype(jnp.bfloat16), "mp").astype(jnp.float32)
    residual_out = ((predicted - target) / math.sqrt(batch_total)).astype(jnp.bfloat16)
    grad_out = sum_at_owner(column_products(current, residual_out).astype(jnp.bfloat16), "dp", 0)
    upstream = jnp.dot(residual_out, w_out.T, preferred_element_type=jnp.float32)
    grads_gain = []
    grads_bias = []
    grads_mid = []
    grad_first = None
    for layer_at in reversed(range(layer_count)):
        normed, inverse, shifted = saved[layer_at]
        slope_a = upstream * mish_slope(shifted)
        bias_sum, gain_sum = together(
            (jnp.sum(slope_a, axis=0), jnp.sum(slope_a * normed, axis=0)), "dp"
        )
        slope_z = (
            bn_gain[layer_at]
            * inverse
            * (slope_a - bias_sum / batch_total - normed * gain_sum / batch_total)
        ).astype(jnp.bfloat16)
        whole_input = full_inputs[layer_at]
        if layer_at == 0:
            grad_first = sum_at_owner(
                column_products(whole_input, slope_z).astype(jnp.bfloat16), "dp", 0
            )
        else:
            grads_mid.append(
                lax.psum_scatter(
                    column_products(whole_input, slope_z).astype(jnp.bfloat16),
                    "dp",
                    scatter_dimension=0,
                    tiled=True,
                ).astype(jnp.float32)
            )
            weights = w_mid[layer_at - 1]
            partial_in = jnp.dot(slope_z, weights.T, preferred_element_type=jnp.float32)
            upstream = lax.psum_scatter(
                partial_in.astype(jnp.bfloat16), "mp", scatter_dimension=1, tiled=True
            ).astype(jnp.float32)
        grads_gain.append(gain_sum)
        grads_bias.append(bias_sum)
    grad_mid = jnp.stack(grads_mid[::-1])
    grad_gain = jnp.stack(grads_gain[::-1])
    grad_bias = jnp.stack(grads_bias[::-1])
    return (grad_first, grad_mid, grad_out, grad_gain, grad_bias)


def solution(mesh):
    return jax.shard_map(
        per_device,
        mesh=mesh,
        in_specs=(
            P("dp"),
            P(),
            P(),
            P(),
            P(),
            P(None, "mp"),
            P(None, None, "mp"),
            P("mp", None),
            P(None, "mp"),
            P(None, "mp"),
            P("dp", None),
        ),
        out_specs=(
            P("dp", "mp"),
            P(None, "dp", "mp"),
            P(("mp", "dp"), None),
            P(None, "mp"),
            P(None, "mp"),
        ),
        check_vma=False,
    )
```

profile of v0, /device:TPU:1, one launch (start us, length us, event | category | flops | bytes accessed | tf_op | source)
XLA Modules:
  0.0 630.7 jit_solution(11090854218543137520)
XLA Ops:
  7.2 0.8 broadcast_compare_fusion
  8.0 0.7 compare_select_fusion.5
  8.7 0.7 compare_reduce_fusion
  9.4 125.3 %fusion.54 = (f32[512]{0:T(512)S(1)}, f32[512]{0:T(512)S(1)}, f32[1024,512]{1,0:T(8,128)S(1)}) fusion(bf16[1024,512]{1,0:T(8,128)(2,1)S(1)} %copy-done, s32[1024]{0:T(1024)S(1)} %bitcast.75, s32[1024]{0:T(1024)S(1)} %bitcast.77, f32[1024]{0:T(1024)S(1)} %get-tuple-element.55, s32[1024]{0:T(1024)} %param.15, s32[1024]{0:T(1024)S(1)} %get-tuple-element.54, ...), kind=kOutput, calls=%fused_computation.121 | convolution fusion | flops 1104673792 | bytes 3181568 | tf_op jit(solution)/shard_map/dot_general | solution.py:88
  134.8 0.9 broadcast_in_dim.34
  135.6 9.6 %all-to-all-start = ((f32[32,1,1024]{2,1,0:T(1,128)}), f32[32,1,1024]{2,1,0:T(1,128)S(1)}, u32[]{:S(2)}, u32[]{:S(2)}) async-start(f32[32,1,1024]{2,1,0:T(1,128)} %broadcast_in_dim.34), calls=%async_computation | async-start | bytes 262144 | tf_op jit(solution)/shard_map/all_to_all | solution.py:13
  145.3 7.5 %all-to-all-done = f32[32,1,1024]{2,1,0:T(1,128)S(1)} async-done(((f32[32,1,1024]{2,1,0:T(1,128)}), f32[32,1,1024]{2,1,0:T(1,128)S(1)}, u32[]{:S(2)}, u32[]{:S(2)}) %all-to-all-start) | async-done | bytes 131104 | tf_op jit(solution)/shard_map/all_to_all | solution.py:13
  152.9 2.5 fusion.21
  155.5 45.6 %all-gather.3.cloned.1.call-done = bf16[1024,2048]{1,0:T(8,128)(2,1)} async-done(((bf16[1024,512]{1,0:T(8,128)(2,1)}), bf16[1024,2048]{1,0:T(8,128)(2,1)}) %all-gather.3.cloned.1.call-update) | async-done | bytes 4194320 | tf_op jit(solution)/shard_map/all_gather | solution.py:90
  201.1 5.2 fusion.53
  206.4 15.3 %all_to_all.51 = f32[32,1,1024]{2,1,0:T(1,128)S(1)} all-to-all(f32[32,1,1024]{2,1,0:T(1,128)S(1)} %broadcast_in_dim.35), channel_id=1, replica_groups=mesh['dp'=32,'mp'=4] {'dp'}, dimensions={0} | all-to-all | bytes 262144 | tf_op jit(solution)/shard_map/all_to_all | solution.py:13
  221.8 2.6 fusion.23
  224.4 44.6 %all-gather.5.cloned.1.call-done = bf16[1024,2048]{1,0:T(8,128)(2,1)} async-done(((bf16[1024,512]{1,0:T(8,128)(2,1)}), bf16[1024,2048]{1,0:T(8,128)(2,1)}) %all-gather.5.cloned.1.call-update) | async-done | bytes 4194320 | tf_op jit(solution)/shard_map/all_gather | solution.py:90
  269.0 6.6 %fusion.52 = (f32[512]{0:T(512)S(1)}, f32[512]{0:T(512)S(1)}, f32[1024,512]{1,0:T(8,128)}) fusion(bf16[1024,2048]{1,0:T(8,128)(2,1)} %all-gather.5.cloned.1.call-done, bf16[2,2048,512]{2,1,0:T(8,128)(2,1)} %param.19), kind=kOutput, calls=%fused_computation.119 | convolution fusion | flops 2149055488 | bytes 8392704 | tf_op jit(solution)/shard_map/dot_general | solution.py:91
  275.7 15.3 %all_to_all.52 = f32[32,1,1024]{2,1,0:T(1,128)S(1)} all-to-all(f32[32,1,1024]{2,1,0:T(1,128)S(1)} %broadcast_in_dim.36), channel_id=1, replica_groups=mesh['dp'=32,'mp'=4] {'dp'}, dimensions={0} | all-to-all | bytes 262144 | tf_op jit(solution)/shard_map/all_to_all | solution.py:13
  291.1 3.1 fusion.25
  294.8 11.6 %all_to_all.53 = bf16[4,1024,64]{1,2,0:T(8,128)(2,1)S(1)} all-to-all(bf16[4,1024,64]{1,2,0:T(8,128)(2,1)S(1)} %broadcast_in_dim.37), channel_id=1, replica_groups=mesh['dp'=32,'mp'=4] {'mp'}, dimensions={0} | all-to-all | bytes 1048576 | tf_op jit(solution)/shard_map/all_to_all | solution.py:13
  306.5 3.7 fusion.51
  310.3 12.6 %all_to_all.54 = f32[32,1,1024]{2,1,0:T(1,128)S(1)} all-to-all(f32[32,1,1024]{2,1,0:T(1,128)S(1)} %broadcast_in_dim.38), channel_id=1, replica_groups=mesh['dp'=32,'mp'=4] {'dp'}, dimensions={0} | all-to-all | bytes 262144 | tf_op jit(solution)/shard_map/all_to_all | solution.py:13
  323.0 3.0 multiply_convert_fusion.2
  326.0 1.0 copy-done.5
  327.0 4.3 convolution_convert_fusion.1
  331.8 42.0 %reduce-scatter.5.cloned.1.call-done = bf16[1024,512]{1,0:T(8,128)(2,1)} async-done(((bf16[1024,2048]{1,0:T(8,128)(2,1)}), bf16[1024,512]{1,0:T(8,128)(2,1)}) %reduce-scatter.5.cloned.1.call-update) | async-done | bytes 1048592 | tf_op jit(solution)/shard_map/reduce_scatter | solution.py:133
  373.8 5.0 fusion.50
  378.9 15.2 %all_to_all.55 = f32[32,1,1024]{2,1,0:T(1,128)S(1)} all-to-all(f32[32,1,1024]{2,1,0:T(1,128)S(1)} %broadcast_in_dim.39), channel_id=1, replica_groups=mesh['dp'=32,'mp'=4] {'dp'}, dimensions={0} | all-to-all | bytes 262144 | tf_op jit(solution)/shard_map/all_to_all | solution.py:13
  394.2 2.3 multiply_convert_fusion.1
  396.5 1.0 copy-done.7
  397.5 4.3 convolution_convert_fusion
  401.9 1.1 copy-done.6
  403.1 5.9 convolution_convert_fusion.2
  409.1 1.1 copy-done.8
  410.2 5.9 convolution_convert_fusion.3
  416.1 28.5 %reduce-scatter.7.cloned.1.call-done = bf16[1024,512]{1,0:T(8,128)(2,1)} async-done(((bf16[1024,2048]{1,0:T(8,128)(2,1)}), bf16[1024,512]{1,0:T(8,128)(2,1)}) %reduce-scatter.7.cloned.1.call-update) | async-done | bytes 1048592 | tf_op jit(solution)/shard_map/reduce_scatter | solution.py:133
  444.7 5.6 fusion.49
  450.3 0.7 broadcast_in_dim.40
  451.0 7.8 %all-to-all-start.6 = ((f32[32,1,1024]{2,1,0:T(1,128)}), f32[32,1,1024]{2,1,0:T(1,128)S(1)}, u32[]{:S(2)}, u32[]{:S(2)}) async-start(f32[32,1,1024]{2,1,0:T(1,128)} %broadcast_in_dim.40), calls=%async_computation.8 | async-start | bytes 262144 | tf_op jit(solution)/shard_map/all_to_all | solution.py:13
  459.2 0.8 reshape.83
  460.0 6.4 %all-to-all-done.6 = f32[32,1,1024]{2,1,0:T(1,128)S(1)} async-done(((f32[32,1,1024]{2,1,0:T(1,128)}), f32[32,1,1024]{2,1,0:T(1,128)S(1)}, u32[]{:S(2)}, u32[]{:S(2)}) %all-to-all-start.6) | async-done | bytes 131104 | tf_op jit(solution)/shard_map/all_to_all | solution.py:13
  466.4 4.1 all-to-all-start.8
  470.6 127.6 %convolution_convert_fusion.4 = bf16[1024,512]{1,0:T(8,128)(2,1)} fusion(f32[1024,512]{1,0:T(8,128)} %get-tuple-element.18, f32[1024,512]{1,0:T(8,128)} %copy-done.3, f32[512]{0:T(512)S(1)} %get-tuple-element.32, f32[512]{0:T(512)S(1)} %get-tuple-element.31, f32[512]{0:T(512)S(1)} %get-tuple-element.40, f32[512]{0:T(512)S(1)} %get-tuple-element.41, ...), kind=kOutput, calls=%fused_computation.65 | convolution fusion | flops 1107820544 | bytes 5284864 | tf_op jit(solution)/shard_map/dot_general | solution.py:74
  598.3 7.5 %all-to-all-start.7 = ((bf16[32,32,512]{2,1,0:T(8,128)(2,1)}), bf16[32,32,512]{2,1,0:T(8,128)(2,1)S(1)}, u32[]{:S(2)}, u32[]{:S(2)}) async-start(bf16[32,32,512]{2,1,0:T(8,128)(2,1)} %bitcast.12), calls=%async_computation.9 | async-start | bytes 2097152 | tf_op jit(solution)/shard_map/all_to_all | solution.py:44
  605.9 0.6 convert_reduce_fusion.2
  606.5 0.6 reduce-scatter.9.cloned.1.call-done
  607.2 1.6 maximum_convert_fusion
  608.8 0.6 pad_maximum_fusion.1
  609.4 0.6 pad_maximum_fusion
  610.0 12.8 %all-to-all-done.7 = bf16[32,32,512]{2,1,0:T(8,128)(2,1)S(1)} async-done(((bf16[32,32,512]{2,1,0:T(8,128)(2,1)}), bf16[32,32,512]{2,1,0:T(8,128)(2,1)S(1)}, u32[]{:S(2)}, u32[]{:S(2)}) %all-to-all-start.7) | async-done | bytes 1048608 | tf_op jit(solution)/shard_map/all_to_all | solution.py:44
  622.8 0.8 convert_reduce_fusion
  (77 shorter events, 3.0 us)
Async XLA Ops:
  7.2 2.2 copy-start
  9.4 135.8 %copy-start.11 = (f32[3,512]{1,0:T(4,128)S(1)}, f32[3,512]{1,0:T(4,128)}, u32[]{:S(2)}) copy-start(f32[3,512]{1,0:T(4,128)} %param.21) | copy-start | bytes 18436
  9.4 135.9 %copy-start.12 = (f32[3,512]{1,0:T(4,128)S(1)}, f32[3,512]{1,0:T(4,128)}, u32[]{:S(2)}) copy-start(f32[3,512]{1,0:T(4,128)} %param.22) | copy-start | bytes 18436
  134.7 20.7 %copy-start.3 = (f32[1024,512]{1,0:T(8,128)}, f32[1024,512]{1,0:T(8,128)S(1)}, u32[]{:S(2)}) copy-start(f32[1024,512]{1,0:T(8,128)S(1)} %get-tuple-element.48) | copy-start | bytes 6291460
  135.6 17.2 %all-to-all-start = ((f32[32,1,1024]{2,1,0:T(1,128)}), f32[32,1,1024]{2,1,0:T(1,128)S(1)}, u32[]{:S(2)}, u32[]{:S(2)}) async-start(f32[32,1,1024]{2,1,0:T(1,128)} %broadcast_in_dim.34), calls=%async_computation | async-start | bytes 262144 | tf_op jit(solution)/shard_map/all_to_all | solution.py:13
  145.2 55.9 %all-gather.3.cloned.1.call-start = ((), (), s32[]{:S(2)}) async-start(), calls=%async_computation.13 | async-start | bytes 5242880 | tf_op jit(solution)/shard_map/all_gather | solution.py:90
  155.5 113.6 %all-gather.5.cloned.1.call-start = ((), (), s32[]{:S(2)}) async-start(), calls=%async_computation.14 | async-start | bytes 5242880 | tf_op jit(solution)/shard_map/all_gather | solution.py:90
  224.4 149.4 %reduce-scatter.5.cloned.1.call-start = ((), (), s32[]{:S(2)}) async-start(), calls=%async_computation.15 | async-start | bytes 5242880 | tf_op jit(solution)/shard_map/reduce_scatter | solution.py:133
  275.6 18.6 %copy-start.10 = (bf16[512,64]{0,1:T(8,128)(2,1)S(1)}, bf16[512,64]{0,1:T(8,128)(2,1)}, u32[]{:S(2)}) copy-start(bf16[512,64]{0,1:T(8,128)(2,1)} %param.20) | copy-start | bytes 196612
  294.2 12.3 %copy-start.1 = (bf16[1024,512]{1,0:T(8,128)(2,1)}, bf16[1024,512]{1,0:T(8,128)(2,1)S(1)}, u32[]{:S(2)}) copy-start(bf16[1024,512]{1,0:T(8,128)(2,1)S(1)} %fusion.25) | copy-start | bytes 3145732
  294.2 12.2 %copy-start.9 = (f32[1024,64]{0,1:T(8,128)S(1)}, f32[1024,64]{0,1:T(8,128)}, u32[]{:S(2)}) copy-start(f32[1024,64]{0,1:T(8,128)} %param.23) | copy-start | bytes 786436
  294.2 12.2 %copy-start.4 = (f32[1024,512]{1,0:T(8,128)S(1)}, f32[1024,512]{1,0:T(8,128)}, u32[]{:S(2)}) copy-start(f32[1024,512]{1,0:T(8,128)} %get-tuple-element.50) | copy-start | bytes 6291460
  323.0 4.0 copy-start.13
  326.0 1.0 copy-start.5
  331.3 113.3 %reduce-scatter.7.cloned.1.call-start = ((), (), s32[]{:S(2)}) async-start(), calls=%async_computation.16 | async-start | bytes 5242880 | tf_op jit(solution)/shard_map/reduce_scatter | solution.py:133
  394.2 3.3 copy-start.14
  396.5 1.0 copy-start.7
  401.9 1.2 copy-start.6
  401.9 204.7 %reduce-scatter.11.cloned.1.call-start = ((), (), s32[]{:S(2)}) async-start(), calls=%async_computation.18 | async-start | bytes 2162688 | tf_op jit(solution)/shard_map/reduce_scatter | solution.py:124
  409.0 1.2 copy-start.8
  409.0 198.2 %reduce-scatter.9.cloned.1.call-start = ((), (), s32[]{:S(2)}) async-start(), calls=%async_computation.17 | async-start | bytes 2162688 | tf_op jit(solution)/shard_map/reduce_scatter | solution.py:124
  416.1 42.7 %copy-start.2 = (bf16[1024,512]{1,0:T(8,128)(2,1)S(1)}, bf16[1024,512]{1,0:T(8,128)(2,1)}, u32[]{:S(2)}) copy-start(bf16[1024,512]{1,0:T(8,128)(2,1)} %copy-done.1) | copy-start | bytes 3145732
  450.3 20.3 %copy-start.15 = (s32[1024]{0:T(1024)S(1)}, s32[1024]{0:T(1024)}, u32[]{:S(2)}) copy-start(s32[1024]{0:T(1024)} %param.15) | copy-start | bytes 12292
  450.3 20.3 %copy-start.16 = (s32[1024]{0:T(1024)S(1)}, s32[1024]{0:T(1024)}, u32[]{:S(2)}) copy-start(s32[1024]{0:T(1024)} %param.13) | copy-start | bytes 12292
  450.3 20.3 %copy-start.17 = (s32[1024]{0:T(1024)S(1)}, s32[1024]{0:T(1024)}, u32[]{:S(2)}) copy-start(s32[1024]{0:T(1024)} %param.14) | copy-start | bytes 12292
  451.0 15.4 %all-to-all-start.6 = ((f32[32,1,1024]{2,1,0:T(1,128)}), f32[32,1,1024]{2,1,0:T(1,128)S(1)}, u32[]{:S(2)}, u32[]{:S(2)}) async-start(f32[32,1,1024]{2,1,0:T(1,128)} %broadcast_in_dim.40), calls=%async_computation.8 | async-start | bytes 262144 | tf_op jit(solution)/shard_map/all_to_all | solution.py:13
  466.4 131.9 %all-to-all-start.8 = ((bf16[32,2,512]{2,1,0:T(2,128)(2,1)}), bf16[32,2,512]{2,1,0:T(2,128)(2,1)S(1)}, u32[]{:S(2)}, u32[]{:S(2)}) async-start(bf16[32,2,512]{2,1,0:T(2,128)(2,1)} %reshape.83), calls=%async_computation.12 | async-start | bytes 131072 | tf_op jit(solution)/shard_map/all_to_all | solution.py:44
  598.3 24.5 %all-to-all-start.7 = ((bf16[32,32,512]{2,1,0:T(8,128)(2,1)}), bf16[32,32,512]{2,1,0:T(8,128)(2,1)S(1)}, u32[]{:S(2)}, u32[]{:S(2)}) async-start(bf16[32,32,512]{2,1,0:T(8,128)(2,1)} %bitcast.12), calls=%async_computation.9 | async-start | bytes 2097152 | tf_op jit(solution)/shard_map/all_to_all | solution.py:44
Sparse Core Ops, SparseCore 0:
  155.6 45.4 all-gather.2
  224.5 44.4 all-gather.4
  331.4 42.3 reduce-scatter.4
  402.0 42.6 reduce-scatter.6
  448.1 77.2 reduce-scatter.10
  528.8 78.3 reduce-scatter.8
where the time goes:
time: 640 us; the launch traced here: 631 us
  matrix products  290 us (45%)
  waiting for transfers between devices  188 us (29%)
  blocking collectives  69.8 us (11%)
  other arithmetic  31.4 us (5%)
  starting transfers between devices  29.6 us (5%)
  between operations  14.7 us (2%)
  local copies, waits for them, and re-layouts  7.28 us (1%)
    dot_general x4, matrix products, column_products(): return jnp.dot(left_rows.T, right_rows, preferred_element_type=jnp.float32)  140 us
    dot_general x1, matrix products, per_device(): summed = jnp.dot(whole_input, w_in, preferred_element_type=jnp.float32)  125 us
    all_gather x2, waiting for transfers between devices, per_device(): whole_input = lax.all_gather(current, 'mp', axis=1, tiled=True)  90.1 us
    reduce_scatter x2, waiting for transfers between devices, per_device(): lax.psum_scatter(partial_in.astype(jnp.bfloat16), 'mp', scatter_dimension...  70.6 us
    all_to_all x5, blocking collectives, from_everyone(): lax.all_to_all(jnp.broadcast_to(array[None], (size, *array.shape)), axis,...  69.8 us
    all_to_all x2, starting transfers between devices, from_everyone(): lax.all_to_all(jnp.broadcast_to(array[None], (size, *array.shape)), axis,...  17.4 us
    all_to_all x2, waiting for transfers between devices, from_everyone(): lax.all_to_all(jnp.broadcast_to(array[None], (size, *array.shape)), axis,...  13.9 us
    all_to_all x2, waiting for transfers between devices, sum_at_owner(): parts = lax.all_to_all(cut_along(array, dim, size), axis, 0, 0, tiled=True)  12.8 us
  transfers between devices with their start and end apart: 10, of which 8 were waited for; matrix products, arithmetic and copies ran while one was open for 24% of the time, Pallas kernels for 0%

commit v1 on v0

--- a/solution.py
+++ b/solution.py
@@ -45,11 +45,26 @@
     return jnp.sum(parts.astype(jnp.float32), axis=0)
 
 
+def float_mod(values, inverse, modulus):
+    rest = values - jnp.floor(values * inverse) * modulus
+    return jnp.where(rest >= modulus, rest - modulus, rest)
+
+
 def encode(ids, hash_a, hash_b, hash_p, hash_m):
-    reduced = ids[:, None] % hash_p[None, :]
-    hashed = (hash_a[None, :] * reduced + hash_b[None, :]) % hash_p[None, :] % hash_m[None, :]
-    scaled = 2.0 * hashed.astype(jnp.float32) / (hash_m[None, :] - 1).astype(jnp.float32) - 1.0
-    return scaled.astype(jnp.bfloat16)
+    modulus = hash_p.astype(jnp.float32)[None, :]
+    buckets = hash_m.astype(jnp.float32)[None, :]
+    below = 1.0 - 2.0**-21
+    inverse_p = below / modulus
+    inverse_m = below / buckets
+    high = (hash_a // 128).astype(jnp.float32)[None, :]
+    low = (hash_a % 128).astype(jnp.float32)[None, :]
+    shift = hash_b.astype(jnp.float32)[None, :]
+    step = 2.0 / (buckets - 1.0)
+    reduced = float_mod(ids.astype(jnp.float32)[:, None], inverse_p, modulus)
+    carried = float_mod(high * reduced, inverse_p, modulus)
+    mixed = float_mod(carried * 128.0 + low * reduced + shift, inverse_p, modulus)
+    hashed = float_mod(mixed, inverse_m, buckets)
+    return lax.optimization_barrier((hashed * step - 1.0).astype(jnp.bfloat16))
 
 
 def mish_act(values):

time: 640 us -> 503 us (0.79); the launches traced: 631 us -> 501 us
  matrix products: 290 us -> 43.4 us
  waiting for transfers between devices: 188 us -> 301 us
  other arithmetic: 31.4 us -> 38.6 us
    dot_general x1, matrix products: 125 us -> 1.28 us  [per_device(): summed = jnp.dot(whole_input, w_in, preferred_element_type=jnp.float32)]
    reduce_scatter x2, waiting for transfers between devices: 0.64 us -> 124 us  [per_device(): lax.psum_scatter(column_products(whole_input, slope_z).astype(jnp.bfloat1...]
    dot_general x4, matrix products: 140 us -> 17.4 us  [column_products(): return jnp.dot(left_rows.T, right_rows, preferred_element_type=jnp.float32)]
    all_to_all x2, waiting for transfers between devices: 12.8 us -> 1.99 us  [sum_at_owner(): parts = lax.all_to_all(cut_along(array, dim, size), axis, 0, 0, tiled=True)]
    convert_element_type x0 -> x6, other arithmetic: none -> 8.75 us  [the longest x1 5.2 us: encode(): return lax.optimization_barrier((hashed * step - 1.0).astype(jnp.bfloat16))]
  transfers between devices with their start and end apart: 10 -> 10, of which waited for: 8 -> 9; matrix products, arithmetic and copies ran while one was open for 24% -> 6% of each run, Pallas kernels for 0% -> 0%
where the time goes in v1:
time: 503 us; the launch traced here: 501 us
  waiting for transfers between devices  301 us (60%)
  blocking collectives  69.8 us (14%)
  matrix products  43.4 us (9%)
  other arithmetic  38.6 us (8%)
  starting transfers between devices  27 us (5%)
  between operations  14.5 us (3%)
  local copies, waits for them, and re-layouts  7.31 us (1%)
    reduce_scatter x2, waiting for transfers between devices, per_device(): lax.psum_scatter(column_products(whole_input, slope_z).astype(jnp.bfloat1...  124 us
    all_gather x2, waiting for transfers between devices, per_device(): whole_input = lax.all_gather(current, 'mp', axis=1, tiled=True)  90.2 us
    reduce_scatter x2, waiting for transfers between devices, per_device(): lax.psum_scatter(partial_in.astype(jnp.bfloat16), 'mp', scatter_dimension...  71 us
    all_to_all x5, blocking collectives, from_everyone(): lax.all_to_all(jnp.broadcast_to(array[None], (size, *array.shape)), axis,...  69.8 us
    dot_general x4, matrix products, column_products(): return jnp.dot(left_rows.T, right_rows, preferred_element_type=jnp.float32)  17.4 us
    all_to_all x2, starting transfers between devices, from_everyone(): lax.all_to_all(jnp.broadcast_to(array[None], (size, *array.shape)), axis,...  17.4 us
    all_to_all x2, waiting for transfers between devices, from_everyone(): lax.all_to_all(jnp.broadcast_to(array[None], (size, *array.shape)), axis,...  13.9 us
    dot_general x2, matrix products, per_device(): jnp.dot(whole_input, w_mid[layer_at - 1], preferred_element_type=jnp.floa...  11.8 us
  transfers between devices with their start and end apart: 10, of which 9 were waited for; matrix products, arithmetic and copies ran while one was open for 6% of the time, Pallas kernels for 0%

profile of v1, /device:TPU:1, one launch (start us, length us, event | category | flops | bytes accessed | tf_op | source)
XLA Modules:
  0.0 501.3 jit_solution(744324461903120079)
XLA Ops:
  7.2 0.8 convert_element_type.82
  8.6 0.7 broadcast_divide_fusion
  9.4 0.7 convert_element_type.81
  10.7 0.7 fusion.31
  11.4 5.2 %fusion.5 = bf16[1024,1024]{1,0:T(8,128)(2,1)S(1)} fusion(f32[1024]{0:T(1024)S(1)} %get-tuple-element.46, f32[1024]{0:T(1024)S(1)} %convert_element_type.85, f32[1024]{0:T(1024)S(1)} %get-tuple-element.45, f32[1024]{0:T(1024)S(1)} %convert_element_type.84, f32[1024]{0:T(1024)S(1)} %get-tuple-element.44, f32[1024]{0:T(1024)S(1)} %convert_element_type.82, ...), kind=kLoop, calls=%fused_computation.12 | loop fusion | flops 37748736 | bytes 2134016 | tf_op jit(solution)/shard_map/convert_element_type | solution.py:67
  16.7 1.3 fusion.44
  18.0 0.8 broadcast_in_dim.20
  18.9 9.6 %all-to-all-start = ((f32[32,1,1024]{2,1,0:T(1,128)}), f32[32,1,1024]{2,1,0:T(1,128)S(1)}, u32[]{:S(2)}, u32[]{:S(2)}) async-start(f32[32,1,1024]{2,1,0:T(1,128)} %broadcast_in_dim.20), calls=%async_computation | async-start | bytes 262144 | tf_op jit(solution)/shard_map/all_to_all | solution.py:13
  28.6 7.5 %all-to-all-done = f32[32,1,1024]{2,1,0:T(1,128)S(1)} async-done(((f32[32,1,1024]{2,1,0:T(1,128)}), f32[32,1,1024]{2,1,0:T(1,128)S(1)}, u32[]{:S(2)}, u32[]{:S(2)}) %all-to-all-start) | async-done | bytes 131104 | tf_op jit(solution)/shard_map/all_to_all | solution.py:13
  36.2 2.5 fusion.16
  38.8 45.5 %all-gather.3.cloned.1.call-done = bf16[1024,2048]{1,0:T(8,128)(2,1)} async-done(((bf16[1024,512]{1,0:T(8,128)(2,1)}), bf16[1024,2048]{1,0:T(8,128)(2,1)}) %all-gather.3.cloned.1.call-update) | async-done | bytes 4194320 | tf_op jit(solution)/shard_map/all_gather | solution.py:105
  84.3 5.2 %fusion.43 = (f32[512]{0:T(512)S(1)}, f32[512]{0:T(512)S(1)}, f32[1024,512]{1,0:T(8,128)S(1)}) fusion(bf16[1024,2048]{1,0:T(8,128)(2,1)} %all-gather.3.cloned.1.call-done, bf16[2,2048,512]{2,1,0:T(8,128)(2,1)} %param.17), kind=kOutput, calls=%fused_computation.112 | convolution fusion | flops 2149055488 | bytes 8392704 | tf_op jit(solution)/shard_map/dot_general | solution.py:106
  89.6 15.3 %all_to_all.51 = f32[32,1,1024]{2,1,0:T(1,128)S(1)} all-to-all(f32[32,1,1024]{2,1,0:T(1,128)S(1)} %broadcast_in_dim.21), channel_id=1, replica_groups=mesh['dp'=32,'mp'=4] {'dp'}, dimensions={0} | all-to-all | bytes 262144 | tf_op jit(solution)/shard_map/all_to_all | solution.py:13
  105.0 2.6 fusion.18
  107.7 44.6 %all-gather.5.cloned.1.call-done = bf16[1024,2048]{1,0:T(8,128)(2,1)} async-done(((bf16[1024,512]{1,0:T(8,128)(2,1)}), bf16[1024,2048]{1,0:T(8,128)(2,1)}) %all-gather.5.cloned.1.call-update) | async-done | bytes 4194320 | tf_op jit(solution)/shard_map/all_gather | solution.py:105
  152.3 6.6 %fusion.42 = (f32[512]{0:T(512)S(1)}, f32[512]{0:T(512)S(1)}, f32[1024,512]{1,0:T(8,128)}) fusion(bf16[1024,2048]{1,0:T(8,128)(2,1)} %all-gather.5.cloned.1.call-done, bf16[2,2048,512]{2,1,0:T(8,128)(2,1)} %param.17), kind=kOutput, calls=%fused_computation.111 | convolution fusion | flops 2149055488 | bytes 8392704 | tf_op jit(solution)/shard_map/dot_general | solution.py:106
  159.0 15.3 %all_to_all.52 = f32[32,1,1024]{2,1,0:T(1,128)S(1)} all-to-all(f32[32,1,1024]{2,1,0:T(1,128)S(1)} %broadcast_in_dim.22), channel_id=1, replica_groups=mesh['dp'=32,'mp'=4] {'dp'}, dimensions={0} | all-to-all | bytes 262144 | tf_op jit(solution)/shard_map/all_to_all | solution.py:13
  174.4 3.1 fusion.20
  178.0 11.6 %all_to_all.53 = bf16[4,1024,64]{1,2,0:T(8,128)(2,1)S(1)} all-to-all(bf16[4,1024,64]{1,2,0:T(8,128)(2,1)S(1)} %broadcast_in_dim.23), channel_id=1, replica_groups=mesh['dp'=32,'mp'=4] {'mp'}, dimensions={0} | all-to-all | bytes 1048576 | tf_op jit(solution)/shard_map/all_to_all | solution.py:13
  189.8 3.7 fusion.41
  193.6 12.6 %all_to_all.54 = f32[32,1,1024]{2,1,0:T(1,128)S(1)} all-to-all(f32[32,1,1024]{2,1,0:T(1,128)S(1)} %broadcast_in_dim.24), channel_id=1, replica_groups=mesh['dp'=32,'mp'=4] {'dp'}, dimensions={0} | all-to-all | bytes 262144 | tf_op jit(solution)/shard_map/all_to_all | solution.py:13
  206.3 3.0 multiply_convert_fusion.2
  209.2 1.0 copy-done.6
  210.2 4.3 convolution_convert_fusion.1
  214.7 42.4 %reduce-scatter.5.cloned.1.call-done = bf16[1024,512]{1,0:T(8,128)(2,1)} async-done(((bf16[1024,2048]{1,0:T(8,128)(2,1)}), bf16[1024,512]{1,0:T(8,128)(2,1)}) %reduce-scatter.5.cloned.1.call-update) | async-done | bytes 1048592 | tf_op jit(solution)/shard_map/reduce_scatter | solution.py:148
  257.1 5.0 fusion.40
  262.2 15.2 %all_to_all.55 = f32[32,1,1024]{2,1,0:T(1,128)S(1)} all-to-all(f32[32,1,1024]{2,1,0:T(1,128)S(1)} %broadcast_in_dim.25), channel_id=1, replica_groups=mesh['dp'=32,'mp'=4] {'dp'}, dimensions={0} | all-to-all | bytes 262144 | tf_op jit(solution)/shard_map/all_to_all | solution.py:13
  277.5 2.3 multiply_convert_fusion.1
  279.8 1.0 copy-done.8
  280.8 4.3 convolution_convert_fusion
  285.2 1.1 copy-done.7
  286.3 5.9 %convolution_convert_fusion.2 = bf16[2048,512]{1,0:T(8,128)(2,1)} fusion(bf16[1024,2048]{1,0:T(8,128)(2,1)} %all-gather.5.cloned.1.call-done, bf16[1024,512]{1,0:T(8,128)(2,1)S(1)} %copy-done.7), kind=kOutput, calls=%fused_computation.15 | convolution fusion | flops 2148532224 | bytes 7340032 | tf_op jit(solution)/shard_map/dot_general | solution.py:89
  292.3 1.1 copy-done.9
  293.5 5.9 %convolution_convert_fusion.3 = bf16[2048,512]{1,0:T(8,128)(2,1)} fusion(bf16[1024,2048]{1,0:T(8,128)(2,1)} %all-gather.3.cloned.1.call-done, bf16[1024,512]{1,0:T(8,128)(2,1)S(1)} %copy-done.9), kind=kOutput, calls=%fused_computation.16 | convolution fusion | flops 2148532224 | bytes 7340032 | tf_op jit(solution)/shard_map/dot_general | solution.py:89
  299.4 28.5 %reduce-scatter.7.cloned.1.call-done = bf16[1024,512]{1,0:T(8,128)(2,1)} async-done(((bf16[1024,2048]{1,0:T(8,128)(2,1)}), bf16[1024,512]{1,0:T(8,128)(2,1)}) %reduce-scatter.7.cloned.1.call-update) | async-done | bytes 1048592 | tf_op jit(solution)/shard_map/reduce_scatter | solution.py:148
  327.9 5.6 %fusion.39 = (f32[512]{0:T(512)S(1)}, f32[512]{0:T(512)S(1)}, f32[1024,512]{1,0:T(8,128)}) fusion(f32[512]{0:T(512)S(1)} %get-tuple-element.35, f32[1024,512]{1,0:T(8,128)} %copy-done.3, f32[512]{0:T(512)S(1)} %get-tuple-element.36, f32[512]{0:T(512)S(1)} %bitcast.57, f32[512]{0:T(512)S(1)} %bitcast.52, bf16[1024,512]{1,0:T(8,128)(2,1)} %reduce-scatter.7.cloned.1.call-done), kind=kLoop, calls=%fused_computation.108 | loop fusion | flops 12057600 | bytes 5255168 | tf_op jit(solution)/shard_map/reduce_sum | solution.py:125
  333.5 0.7 broadcast_in_dim.26
  334.3 7.8 %all-to-all-start.6 = ((f32[32,1,1024]{2,1,0:T(1,128)}), f32[32,1,1024]{2,1,0:T(1,128)S(1)}, u32[]{:S(2)}, u32[]{:S(2)}) async-start(f32[32,1,1024]{2,1,0:T(1,128)} %broadcast_in_dim.26), calls=%async_computation.8 | async-start | bytes 262144 | tf_op jit(solution)/shard_map/all_to_all | solution.py:13
  342.5 0.8 reshape.83
  343.2 6.4 %all-to-all-done.6 = f32[32,1,1024]{2,1,0:T(1,128)S(1)} async-done(((f32[32,1,1024]{2,1,0:T(1,128)}), f32[32,1,1024]{2,1,0:T(1,128)S(1)}, u32[]{:S(2)}, u32[]{:S(2)}) %all-to-all-start.6) | async-done | bytes 131104 | tf_op jit(solution)/shard_map/all_to_all | solution.py:13
  349.6 3.9 all-to-all-start.8
  353.7 5.3 %convolution_convert_fusion.4 = bf16[1024,512]{1,0:T(8,128)(2,1)} fusion(bf16[1024,1024]{1,0:T(8,128)(2,1)} %copy-done.5, f32[1024,512]{1,0:T(8,128)} %get-tuple-element.17, f32[1024,512]{1,0:T(8,128)} %copy-done.3, f32[512]{0:T(512)S(1)} %get-tuple-element.27, f32[512]{0:T(512)S(1)} %get-tuple-element.26, f32[512]{0:T(512)S(1)} %get-tuple-element.35, ...), kind=kOutput, calls=%fused_computation.58 | convolution fusion | flops 1078460416 | bytes 7350272 | tf_op jit(solution)/shard_map/dot_general | solution.py:89
  359.0 2.0 all-to-all-done.8
  361.0 5.5 %all-to-all-start.7 = ((bf16[32,32,512]{2,1,0:T(8,128)(2,1)}), bf16[32,32,512]{2,1,0:T(8,128)(2,1)S(1)}, u32[]{:S(2)}, u32[]{:S(2)}) async-start(bf16[32,32,512]{2,1,0:T(8,128)(2,1)} %bitcast.8), calls=%async_computation.9 | async-start | bytes 2097152 | tf_op jit(solution)/shard_map/all_to_all | solution.py:44
  367.3 41.7 %reduce-scatter.11.cloned.1.call-done = bf16[64,512]{1,0:T(8,128)(2,1)} async-done(((bf16[2048,512]{1,0:T(8,128)(2,1)}), bf16[64,512]{1,0:T(8,128)(2,1)}) %reduce-scatter.11.cloned.1.call-update) | async-done | bytes 65552 | tf_op jit(solution)/shard_map/reduce_scatter | solution.py:139
  409.0 81.9 %reduce-scatter.9.cloned.1.call-done = bf16[64,512]{1,0:T(8,128)(2,1)} async-done(((bf16[2048,512]{1,0:T(8,128)(2,1)}), bf16[64,512]{1,0:T(8,128)(2,1)}) %reduce-scatter.9.cloned.1.call-update) | async-done | bytes 65552 | tf_op jit(solution)/shard_map/reduce_scatter | solution.py:139
  490.8 1.6 maximum_convert_fusion
  493.6 0.8 convert_reduce_fusion
  (77 shorter events, 5.8 us)
Async XLA Ops:
  7.2 9.5 %copy-start = (bf16[1024,512]{1,0:T(8,128)(2,1)S(1)}, bf16[1024,512]{1,0:T(8,128)(2,1)}, u32[]{:S(2)}) copy-start(bf16[1024,512]{1,0:T(8,128)(2,1)} %param.16) | copy-start | bytes 3145732
  16.7 1.4 copy-start.5
  16.7 11.9 %copy-start.12 = (f32[3,512]{1,0:T(4,128)S(1)}, f32[3,512]{1,0:T(4,128)}, u32[]{:S(2)}) copy-start(f32[3,512]{1,0:T(4,128)} %param.19) | copy-start | bytes 18436
  16.7 11.9 %copy-start.13 = (f32[3,512]{1,0:T(4,128)S(1)}, f32[3,512]{1,0:T(4,128)}, u32[]{:S(2)}) copy-start(f32[3,512]{1,0:T(4,128)} %param.20) | copy-start | bytes 18436
  18.0 20.7 %copy-start.3 = (f32[1024,512]{1,0:T(8,128)}, f32[1024,512]{1,0:T(8,128)S(1)}, u32[]{:S(2)}) copy-start(f32[1024,512]{1,0:T(8,128)S(1)} %get-tuple-element.47) | copy-start | bytes 6291460
  18.9 17.2 %all-to-all-start = ((f32[32,1,1024]{2,1,0:T(1,128)}), f32[32,1,1024]{2,1,0:T(1,128)S(1)}, u32[]{:S(2)}, u32[]{:S(2)}) async-start(f32[32,1,1024]{2,1,0:T(1,128)} %broadcast_in_dim.20), calls=%async_computation | async-start | bytes 262144 | tf_op jit(solution)/shard_map/all_to_all | solution.py:13
  28.5 55.9 %all-gather.3.cloned.1.call-start = ((), (), s32[]{:S(2)}) async-start(), calls=%async_computation.13 | async-start | bytes 5242880 | tf_op jit(solution)/shard_map/all_gather | solution.py:105
  38.7 113.6 %all-gather.5.cloned.1.call-start = ((), (), s32[]{:S(2)}) async-start(), calls=%async_computation.14 | async-start | bytes 5242880 | tf_op jit(solution)/shard_map/all_gather | solution.py:105
  107.7 149.4 %reduce-scatter.5.cloned.1.call-start = ((), (), s32[]{:S(2)}) async-start(), calls=%async_computation.15 | async-start | bytes 5242880 | tf_op jit(solution)/shard_map/reduce_scatter | solution.py:148
  158.9 18.6 %copy-start.11 = (bf16[512,64]{0,1:T(8,128)(2,1)S(1)}, bf16[512,64]{0,1:T(8,128)(2,1)}, u32[]{:S(2)}) copy-start(bf16[512,64]{0,1:T(8,128)(2,1)} %param.18) | copy-start | bytes 196612
  177.5 12.3 %copy-start.1 = (bf16[1024,512]{1,0:T(8,128)(2,1)}, bf16[1024,512]{1,0:T(8,128)(2,1)S(1)}, u32[]{:S(2)}) copy-start(bf16[1024,512]{1,0:T(8,128)(2,1)S(1)} %fusion.20) | copy-start | bytes 3145732
  177.5 12.2 %copy-start.10 = (f32[1024,64]{0,1:T(8,128)S(1)}, f32[1024,64]{0,1:T(8,128)}, u32[]{:S(2)}) copy-start(f32[1024,64]{0,1:T(8,128)} %param.21) | copy-start | bytes 786436
  177.5 12.2 %copy-start.4 = (f32[1024,512]{1,0:T(8,128)S(1)}, f32[1024,512]{1,0:T(8,128)}, u32[]{:S(2)}) copy-start(f32[1024,512]{1,0:T(8,128)} %get-tuple-element.49) | copy-start | bytes 6291460
  206.3 4.0 copy-start.14
  209.2 1.0 copy-start.6
  214.6 113.3 %reduce-scatter.7.cloned.1.call-start = ((), (), s32[]{:S(2)}) async-start(), calls=%async_computation.16 | async-start | bytes 5242880 | tf_op jit(solution)/shard_map/reduce_scatter | solution.py:148
  277.4 3.3 copy-start.15
  279.8 1.0 copy-start.8
  285.1 1.2 copy-start.7
  285.2 123.8 %reduce-scatter.11.cloned.1.call-start = ((), (), s32[]{:S(2)}) async-start(), calls=%async_computation.18 | async-start | bytes 2162688 | tf_op jit(solution)/shard_map/reduce_scatter | solution.py:139
  292.3 1.2 copy-start.9
  292.3 198.5 %reduce-scatter.9.cloned.1.call-start = ((), (), s32[]{:S(2)}) async-start(), calls=%async_computation.17 | async-start | bytes 2162688 | tf_op jit(solution)/shard_map/reduce_scatter | solution.py:139
  299.4 42.6 %copy-start.2 = (bf16[1024,512]{1,0:T(8,128)(2,1)S(1)}, bf16[1024,512]{1,0:T(8,128)(2,1)}, u32[]{:S(2)}) copy-start(bf16[1024,512]{1,0:T(8,128)(2,1)} %copy-done.1) | copy-start | bytes 3145732
  334.3 15.4 %all-to-all-start.6 = ((f32[32,1,1024]{2,1,0:T(1,128)}), f32[32,1,1024]{2,1,0:T(1,128)S(1)}, u32[]{:S(2)}, u32[]{:S(2)}) async-start(f32[32,1,1024]{2,1,0:T(1,128)} %broadcast_in_dim.26), calls=%async_computation.8 | async-start | bytes 262144 | tf_op jit(solution)/shard_map/all_to_all | solution.py:13
  349.6 11.4 %all-to-all-start.8 = ((bf16[32,2,512]{2,1,0:T(2,128)(2,1)}), bf16[32,2,512]{2,1,0:T(2,128)(2,1)S(1)}, u32[]{:S(2)}, u32[]{:S(2)}) async-start(bf16[32,2,512]{2,1,0:T(2,128)(2,1)} %reshape.83), calls=%async_computation.12 | async-start | bytes 131072 | tf_op jit(solution)/shard_map/all_to_all | solution.py:44
  361.0 132.6 %all-to-all-start.7 = ((bf16[32,32,512]{2,1,0:T(8,128)(2,1)}), bf16[32,32,512]{2,1,0:T(8,128)(2,1)S(1)}, u32[]{:S(2)}, u32[]{:S(2)}) async-start(bf16[32,32,512]{2,1,0:T(8,128)(2,1)} %bitcast.8), calls=%async_computation.9 | async-start | bytes 2097152 | tf_op jit(solution)/shard_map/all_to_all | solution.py:44
Sparse Core Ops, SparseCore 0:
  38.9 45.4 all-gather.2
  107.8 44.4 all-gather.4
  214.7 42.3 reduce-scatter.4
  285.3 42.6 reduce-scatter.6
  331.3 77.5 reduce-scatter.10
  412.4 78.4 reduce-scatter.8
